TPU v7x, 32 devices: a whole 2x2x4 slice. The times are simulated.
32 devices in a mesh: gx: 4 (over y, core), gy: 8 (over z, x).
Axes of the slice: x: 2, y: 2, z: 4, core: 2. Of those that a mesh axis runs over, the one named last changes fastest.
Arguments:
- pool_old: float32 [40, 131072], P(None, ('gx', 'gy')), may hold values from 0.5 to 2
- pool_new: float32 [40, 131072], P(None, ('gx', 'gy')), may hold values from 0.5 to 2
- flux: float32 [40, 131072], P(None, ('gx', 'gy')), may hold values from -6 to 6
- area: float32 [131072], P(('gx', 'gy')), may hold values from 0.05 to 1
- pft_id: int32 [131072], P(('gx', 'gy')), may hold values from 0 to 78
- region_id: int32 [131072], P(('gx', 'gy')), may hold values from 0 to 31, as said below
Outputs:
- pool_totals: float32 [40, 2528], replicated
- error_totals: float32 [40, 2528], replicated
Inputs may be any that keep to these rules, and one draw needn't show every extreme that they name: `region_id`: patch i lies in block k = i // 4096; with K = 32 blocks, its region is (k * 32) // K or ((k * 32) // K + 1) mod 32.
All inputs are finite; a program needn't handle non-finite values.
Results may differ from a plain program's by a relative error of at most 0.000076.
Values sent between devices are 32-bit elements; how exact they have to be, the bound alone decides.
A program may use at most 64 MiB of HBM per device.

v0:
```python
import jax
import jax.numpy as jnp
from jax import lax
from jax.sharding import PartitionSpec as P

POOLS = 40
PFT = 79
REGION = 32
CELLS = 2528


def shards(pool_old, pool_new, flux, area, pft_id, region_id):
    width_x = lax.axis_size("gx")
    width_y = lax.axis_size("gy")
    devices_all = width_x * width_y
    position = lax.axis_index("gx") * width_y + lax.axis_index("gy")
    base = position * REGION // devices_all
    offset_here = (region_id - base) % REGION
    compact_cell = pft_id * 2 + offset_here
    stored = area[None, :] * pool_new
    balance = area[None, :] * (pool_new - pool_old - 0.5 * flux)
    stacked = jnp.concatenate([stored, balance], axis=0)
    rows = stacked.shape[0]
    patch_count = stacked.shape[1]
    block = min(512, patch_count)
    blocks = patch_count // block
    stacked_blocks = stacked.reshape(rows, blocks, block).transpose(1, 0, 2)
    cell_blocks = compact_cell.reshape(blocks, block)
    columns = jnp.arange(2 * PFT, dtype=jnp.int32)

    def accumulate(totals, inputs):
        values, cells_here = inputs
        onehot = (cells_here[:, None] == columns[None, :]).astype(jnp.float32)
        added = jnp.dot(
            values, onehot, preferred_element_type=jnp.float32, precision=lax.Precision.HIGHEST
        )
        return (totals + added, None)

    local_table, _ = lax.scan(
        accumulate, jnp.zeros((rows, 2 * PFT), jnp.float32), (stacked_blocks, cell_blocks)
    )
    local_table = local_table.reshape(rows, PFT, 2)
    region_axis = jnp.arange(REGION, dtype=jnp.int32)
    pair_axis = jnp.arange(2, dtype=jnp.int32)
    span = REGION // width_x + 1
    start = lax.axis_index("gx") * (REGION // width_x)
    span_axis = jnp.arange(span, dtype=jnp.int32)
    into_group = ((base - start + pair_axis)[:, None] == span_axis[None, :]).astype(jnp.float32)
    group_table = jnp.einsum(
        "apj,jw->apw", local_table, into_group, precision=lax.Precision.HIGHEST
    )
    group_total = lax.psum(group_table, "gy")
    into_full = (((start + span_axis) % REGION)[:, None] == region_axis[None, :]).astype(
        jnp.float32
    )
    placed = jnp.einsum("apw,wr->apr", group_total, into_full, precision=lax.Precision.HIGHEST)
    totals = lax.psum(placed.reshape(rows, CELLS), "gx")
    patch_all = patch_count * devices_all
    totals = totals * jnp.float32(CELLS / patch_all)
    return (totals[:POOLS], totals[POOLS:])


def solution(mesh):
    return jax.shard_map(
        shards,
        mesh=mesh,
        in_specs=(
            P(None, ("gx", "gy")),
            P(None, ("gx", "gy")),
            P(None, ("gx", "gy")),
            P(("gx", "gy")),
            P(("gx", "gy")),
            P(("gx", "gy")),
        ),
        out_specs=(P(), P()),
        check_vma=False,
    )
```

profile of v0, /device:TPU:0, one launch (start us, length us, event | category | flops | bytes accessed | tf_op | source)
XLA Modules:
  0.0 140.4 jit_solution(4403642553132659175)
XLA Ops:
  7.2 0.8 fusion.4
  8.0 1.6 %broadcast_multiply_fusion.1 = (f32[40,4096]{1,0:T(8,128)S(1)}, f32[40,4096]{1,0:T(8,128)S(1)}) fusion(f32[40,4096]{1,0:T(8,128)} %param.9, f32[4096]{0:T(1024)} %param.11, f32[40,4096]{1,0:T(8,128)} %param.10, f32[40,4096]{1,0:T(8,128)} %param.8), kind=kLoop, calls=%fused_computation.10 | loop fusion | flops 819200 | bytes 3293184 | tf_op jit(solution)/shard_map/mul | solution.py:20
  9.7 0.8 copy.13
  10.6 4.8 %while.11 = (s32[]{:T(128)}, f32[80,158]{1,0:T(8,128)S(1)}, f32[8,80,512]{2,0,1:T(8,128)S(1)}, s32[8,512]{1,0:T(8,128)S(1)}, s32[]{:T(128)}, /*index=5*/s32[]{:T(128)}) while((s32[]{:T(128)}, f32[80,158]{1,0:T(8,128)S(1)}, f32[8,80,512]{2,0,1:T(8,128)S(1)}, s32[8,512]{1,0:T(8,128)S(1)}, s32[]{:T(128)}, /*index=5*/s32[]{:T(128)}) %tuple.36), condition=%wide.region_1.2_spmd.clone, body=%wide.region_0.1_spmd.clone.sunk | while | flops 77766336 | bytes 598871 | solution.py:39
  10.6 0.1 constant_dynamic-slice_fusion.5
  10.8 0.4 convolution_add_fusion.2
  11.2 0.1 constant_dynamic-slice_fusion.5
  11.4 0.4 convolution_add_fusion.2
  11.8 0.1 constant_dynamic-slice_fusion.5
  12.0 0.4 convolution_add_fusion.2
  12.4 0.1 constant_dynamic-slice_fusion.5
  12.5 0.4 convolution_add_fusion.2
  13.0 0.1 constant_dynamic-slice_fusion.5
  13.1 0.4 convolution_add_fusion.2
  13.7 0.4 convolution_add_fusion.2
  14.3 0.4 convolution_add_fusion.2
  14.9 0.4 convolution_add_fusion.2
  15.5 1.4 fusion.9
  17.0 76.4 %all-reduce.3.cloned.1.call-done = f32[80,79,9]{0,2,1:T(8,128)} async-done(((f32[80,79,9]{0,2,1:T(8,128)}), f32[80,79,9]{0,2,1:T(8,128)}) %all-reduce.3.cloned.1.call-update) | async-done | bytes 227536 | tf_op jit(solution)/shard_map/psum | solution.py:52
  93.4 1.9 %fusion.6 = f32[80,79,32]{0,2,1:T(8,128)S(1)} fusion(f32[80,79,9]{0,2,1:T(8,128)} %all-reduce.3.cloned.1.call-done, s32[9]{0:T(128)S(1)} %and_select_fusion), kind=kOutput, calls=%fused_computation.18 | convolution fusion | flops 21842208 | bytes 1036516 | tf_op jit(solution)/shard_map/apw,wr->apr/dot_general | solution.py:56
  95.3 1.3 copy.11
  96.6 34.8 %all-reduce.5.cloned.1.call-done = f32[80,2528]{1,0:T(8,128)} async-done(((f32[80,2528]{1,0:T(8,128)}), f32[80,2528]{1,0:T(8,128)}) %all-reduce.5.cloned.1.call-update) | async-done | bytes 808976 | tf_op jit(solution)/shard_map/psum | solution.py:57
  131.4 1.2 broadcast_multiply_fusion
  132.7 0.9 fusion.15
  (22 shorter events, 0.9 us)
Async XLA Ops:
  7.2 86.3 %all-reduce.3.cloned.1.call-start = ((), (), s32[]{:S(2)}) async-start(), calls=%async_computation | async-start | bytes 1294336 | tf_op jit(solution)/shard_map/psum | solution.py:52
  16.9 114.5 %all-reduce.5.cloned.1.call-start = ((), (), s32[]{:S(2)}) async-start(), calls=%async_computation.1 | async-start | bytes 1638400 | tf_op jit(solution)/shard_map/psum | solution.py:57
Sparse Core Ops, SparseCore 0:
  17.0 76.3 all-reduce.2
  96.7 34.6 all-reduce.4
where the time goes:
time: 141 us; the launch traced here: 140 us
  waiting for transfers between devices  111 us (79%)
  between operations  14.1 us (10%)
  matrix products  6.42 us (5%)
  local copies, waits for them, and re-layouts  4.48 us (3%)
  other arithmetic  3.68 us (3%)
    psum x1, waiting for transfers between devices, shards(): group_total = lax.psum(group_table, 'gy')  76.4 us
    psum x1, waiting for transfers between devices, shards(): totals = lax.psum(placed.reshape(rows, CELLS), 'gx')  34.8 us
    dot_general x8, matrix products, accumulate(): jnp.dot(values, onehot, preferred_element_type=jnp.float32, precision=lax...  3.17 us
  transfers between devices with their start and end apart: 2, of which 2 were waited for; matrix products, arithmetic and copies ran while one was open for 0% of the time, Pallas kernels for 0%

commit v1 on v0

--- a/solution.py
+++ b/solution.py
@@ -1,12 +1,212 @@
+import functools
 import jax
 import jax.numpy as jnp
 from jax import lax
+from jax.experimental import pallas as pl
+from jax.experimental.pallas import tpu as pltpu
 from jax.sharding import PartitionSpec as P
 
 POOLS = 40
 PFT = 79
 REGION = 32
 CELLS = 2528
+MESH = pl.DeviceIdType.MESH
+ROWS = 2 * POOLS
+PFT_PAD = 80
+MAIN = 56
+REST = PFT_PAD - MAIN
+LANES = 128
+SPARE = LANES - ROWS
+BLOCKS = 4
+
+
+def pack(table):
+    main = table[:MAIN]
+    rest = table[MAIN:]
+    lane = lax.broadcasted_iota(jnp.int32, (REST, LANES), 1)
+    first = pltpu.roll(rest, ROWS, 1)
+    second = pltpu.roll(rest, ROWS - SPARE, 1)
+    top = jnp.where(lane < ROWS, main[:REST], first)
+    middle = jnp.where(lane < ROWS, main[REST : 2 * REST], second)
+    return jnp.concatenate([top, middle, main[2 * REST :]], axis=0)
+
+
+def kernel(
+    zs, ys, scale,
+    old_hbm, new_hbm, flux_hbm, area_ref, pft_ref, region_ref,
+    stored_ref, error_ref,
+    old_v, new_v, flux_v, nxt, halo, gathered,
+    in_sem, halo_send, halo_recv, send_sem, recv_sem,
+):
+    gx, gy = lax.axis_index("gx"), lax.axis_index("gy")
+    ny = 2 * zs
+    devices = 2 * ys * ny
+    patches = area_ref.shape[1]
+    width = patches // BLOCKS
+    y, c = gx // 2, gx % 2
+    z, x = gy // 2, gy % 2
+    me = gx * ny + gy
+    copies = []
+    for k in range(BLOCKS):
+        part = pl.ds(k * width, width)
+        for a, (src, dst) in enumerate(((new_hbm, new_v), (old_hbm, old_v), (flux_hbm, flux_v))):
+            copy = pltpu.make_async_copy(src.at[:, part], dst.at[:, part], in_sem.at[a, k])
+            copy.start()
+            copies.append(copy)
+
+    def dev(y_, c_, z_, x_):
+        return (y_ * 2 + c_, z_ * 2 + x_)
+
+    def slot(y_, c_, z_, x_):
+        return (y_ * 2 + c_) * ny + z_ * 2 + x_
+
+    after = lax.rem(me + 1, devices)
+    before = lax.rem(me + devices - 1, devices)
+    dev_after = (after // ny, lax.rem(after, ny))
+    dev_before = (before // ny, lax.rem(before, ny))
+    z_peers = [lax.rem(z + k, zs) for k in range(1, zs)]
+    dev_x, dev_y, dev_c = dev(y, c, z, 1 - x), dev(1 - y, c, z, x), dev(y, 1 - c, z, x)
+    partners = [dev(y, c, q, x) for q in z_peers] + [dev_x, dev_y, dev_c, dev_after, dev_before]
+    barrier = pltpu.get_barrier_semaphore()
+    for partner in partners:
+        pl.semaphore_signal(barrier, inc=1, device_id=partner, device_id_type=MESH)
+
+    base = me * REGION // devices
+    total = None
+    for k in range(BLOCKS):
+        part = pl.ds(k * width, width)
+        code = pft_ref[:, part] + jnp.where(region_ref[:, part] == base, 0, PFT_PAD)
+        cells = lax.broadcasted_iota(jnp.int32, (2 * PFT_PAD, width), 0)
+        hot = jnp.where(cells == code, 1.0, 0.0).astype(jnp.bfloat16)
+        for copy in copies[3 * k : 3 * k + 3]:
+            copy.wait()
+        area = area_ref[:, part]
+        new = new_v[:, part]
+        stored = area * new
+        balance = area * (new - old_v[:, part] - 0.5 * flux_v[:, part])
+        values = jnp.concatenate([stored, balance], axis=0)
+        high = values.astype(jnp.bfloat16)
+        left = values - high.astype(jnp.float32)
+        middle = left.astype(jnp.bfloat16)
+        low = (left - middle.astype(jnp.float32)).astype(jnp.bfloat16)
+        pieces = jnp.concatenate([high, middle, low], axis=0)
+        added = lax.dot_general(hot, pieces, (((1,), (1,)), ((), ())), preferred_element_type=jnp.float32)
+        total = added if total is None else total + added
+    wide = jnp.concatenate([total, jnp.zeros((2 * PFT_PAD, 2 * LANES - 3 * ROWS), jnp.float32)], axis=1)
+    first = wide[:, :LANES]
+    second = wide[:, LANES:]
+    lane = lax.broadcasted_iota(jnp.int32, (2 * PFT_PAD, LANES), 1)
+    mid = jnp.where(lane < LANES - ROWS, pltpu.roll(first, LANES - ROWS, 1), pltpu.roll(second, LANES - ROWS, 1))
+    last = pltpu.roll(second, 2 * LANES - 2 * ROWS, 1)
+    table = (first + mid + last) * scale
+    own = pack(table[:PFT_PAD])
+    nxt[...] = pack(table[PFT_PAD:])
+
+    pl.semaphore_wait(barrier, len(partners))
+    halo_copy = pltpu.make_async_remote_copy(
+        src_ref=nxt, dst_ref=halo, send_sem=halo_send, recv_sem=halo_recv,
+        device_id=dev_after, device_id_type=MESH,
+    )
+    halo_copy.start()
+    halo_copy.wait_recv()
+
+    def chunk(s):
+        return gathered.at[pl.ds(pl.multiple_of(s * MAIN, 8), MAIN), :]
+
+    gathered[pl.ds(pl.multiple_of(me * MAIN, 8), MAIN), :] = own + halo[...]
+    sent = []
+
+    def send(s, target):
+        copy = pltpu.make_async_remote_copy(
+            src_ref=chunk(s), dst_ref=chunk(s), send_sem=send_sem.at[len(sent)],
+            recv_sem=recv_sem.at[s], device_id=target, device_id_type=MESH,
+        )
+        copy.start()
+        sent.append(copy)
+
+    def arrive(s):
+        pltpu.make_async_remote_copy(
+            src_ref=chunk(s), dst_ref=chunk(s), send_sem=send_sem.at[0],
+            recv_sem=recv_sem.at[s], device_id=dev_x, device_id_type=MESH,
+        ).wait_recv()
+
+    send(me, dev_y)
+    send(me, dev_x)
+    for q in z_peers:
+        send(me, dev(y, c, q, x))
+    send(me, dev_c)
+    for q in z_peers:
+        s = slot(y, c, q, x)
+        arrive(s)
+        send(s, dev_y)
+        send(s, dev_x)
+        send(s, dev_c)
+    for k, q in enumerate([z] + z_peers):
+        s = slot(y, c, q, 1 - x)
+        arrive(s)
+        if k % 2 == 0:
+            send(s, dev_y)
+        send(s, dev_c)
+        s = slot(1 - y, c, q, x)
+        arrive(s)
+        if k % 2 == 1:
+            send(s, dev_x)
+        send(s, dev_c)
+    for q in [z] + z_peers:
+        s = slot(1 - y, c, q, 1 - x)
+        arrive(s)
+        send(s, dev_c)
+    for q in [z] + z_peers:
+        for y_, x_ in ((y, x), (y, 1 - x), (1 - y, x), (1 - y, 1 - x)):
+            arrive(slot(y_, 1 - c, q, x_))
+    halo_copy.wait_send()
+    for copy in sent:
+        copy.wait_send()
+
+    for u in range(MAIN // 4):
+        rows = [gathered[pl.ds(4 * u + j, REGION, stride=MAIN), :] for j in range(4)]
+        tile = jnp.concatenate(rows, axis=0).T
+        here = pl.ds(u * LANES, LANES)
+        stored_ref[:, here] = tile[:POOLS]
+        error_ref[:, here] = tile[POOLS:ROWS]
+        if 4 * u < 2 * REST:
+            t = (MAIN // 4) + (u if 4 * u < REST else u - REST // 4)
+            w = min(LANES, CELLS - t * LANES)
+            there = pl.ds(t * LANES, w)
+            if 4 * u < REST:
+                stored_ref[:, there] = tile[ROWS : ROWS + POOLS, :w]
+                error_ref[: SPARE - POOLS, there] = tile[ROWS + POOLS :, :w]
+            else:
+                error_ref[SPARE - POOLS :, there] = tile[ROWS : 2 * ROWS - SPARE, :w]
+
+
+def kernel_shards(zs, ys, pool_old, pool_new, flux, area, pft_id, region_id):
+    patches = area.shape[0]
+    devices = 4 * ys * zs
+    scale = CELLS / (patches * devices)
+    out = jax.ShapeDtypeStruct((POOLS, CELLS), jnp.float32)
+    hbm, vmem = pl.BlockSpec(memory_space=pl.ANY), pl.BlockSpec(memory_space=pltpu.VMEM)
+    sends = 3 + zs - 1 + 3 * (zs - 1) + 3 * zs + zs
+    return pl.pallas_call(
+        functools.partial(kernel, zs, ys, scale),
+        out_shape=(out, out),
+        in_specs=[hbm] * 3 + [vmem] * 3,
+        out_specs=(vmem, vmem),
+        scratch_shapes=[
+            pltpu.VMEM((POOLS, patches), jnp.float32),
+            pltpu.VMEM((POOLS, patches), jnp.float32),
+            pltpu.VMEM((POOLS, patches), jnp.float32),
+            pltpu.VMEM((MAIN, LANES), jnp.float32),
+            pltpu.VMEM((MAIN, LANES), jnp.float32),
+            pltpu.VMEM((REGION * MAIN, LANES), jnp.float32),
+            pltpu.SemaphoreType.DMA((3, BLOCKS)),
+            pltpu.SemaphoreType.DMA,
+            pltpu.SemaphoreType.DMA,
+            pltpu.SemaphoreType.DMA((sends,)),
+            pltpu.SemaphoreType.DMA((devices,)),
+        ],
+        compiler_params=pltpu.CompilerParams(collective_id=0, has_side_effects=True),
+    )(pool_old, pool_new, flux, area[None, :], pft_id[None, :], region_id[None, :])
 
 
 def shards(pool_old, pool_new, flux, area, pft_id, region_id):
@@ -61,8 +261,13 @@
 
 
 def solution(mesh):
+    wide, deep = mesh.shape["gx"], mesh.shape["gy"]
+    if wide == 4 and wide * deep == REGION:
+        local = functools.partial(kernel_shards, deep // 2, wide // 2)
+    else:
+        local = shards
     return jax.shard_map(
-        shards,
+        local,
         mesh=mesh,
         in_specs=(
             P(None, ("gx", "gy")),

time: 141 us -> 26.8 us (0.19)
  the two profiles are of different devices: /device:TPU:0 before, /device:TPU:27 now
where the time goes in v1:
time: 26.8 us; the launch traced here: 26.5 us
  Pallas kernels  23.2 us (87%)
  local copies, waits for them, and re-layouts  2.59 us (10%)
  between operations  0.65 us (2%)
    pallas_call x1, Pallas kernels, kernel_shards(): pl.pallas_call(functools.partial(kernel, zs, ys, scale), out_shape=(out,...  23.2 us
    unnamed x4, local copies, waits for them, and re-layouts  2.59 us

profile of v1, /device:TPU:27, one launch (start us, length us, event | category | flops | bytes accessed | tf_op | source)
XLA Modules:
  0.0 26.5 jit_solution(3386559619062379210)
XLA Ops:
  0.6 23.2 %shard_map.77 = (f32[40,2528]{1,0:T(8,128)}, f32[40,2528]{1,0:T(8,128)}) custom-call(f32[40,4096]{1,0:T(8,128)} %old_hbm.1, f32[40,4096]{1,0:T(8,128)} %new_hbm.1, f32[40,4096]{1,0:T(8,128)} %flux_hbm.1, f32[1,4096]{1,0:T(1,128)} %bitcast.3, s32[1,4096]{1,0:T(1,128)} %bitcast.4, s32[1,4096]{1,0:T(1,128)} %bitcast.5), custom_call_target="tpu_custom_call" | custom-call | tf_op jit(solution)/shard_map/pallas_call | solution.py:190
  23.9 0.0 copy-start
  23.9 1.8 %copy.10 = f32[40,2528]{1,0:T(8,128)} copy(f32[40,2528]{1,0:T(8,128)} %get-tuple-element.4) | data formatting | bytes 808960
  25.7 0.0 copy-done
  25.7 0.8 %copy.11 = f32[40,2528]{1,0:T(8,128)} copy(f32[40,2528]{1,0:T(8,128)S(1)} %copy-done) | data formatting | bytes 808960
Async XLA Ops:
  23.9 1.8 %copy-start = (f32[40,2528]{1,0:T(8,128)S(1)}, f32[40,2528]{1,0:T(8,128)}, u32[]{:S(2)}) copy-start(f32[40,2528]{1,0:T(8,128)} %get-tuple-element.5) | copy-start | bytes 1213444

commit v2 on v1

--- a/solution.py
+++ b/solution.py
@@ -35,7 +35,7 @@
     zs, ys, scale,
     old_hbm, new_hbm, flux_hbm, area_ref, pft_ref, region_ref,
     stored_ref, error_ref,
-    old_v, new_v, flux_v, nxt, halo, gathered,
+    old_v, new_v, flux_v, own, nxt, theirs, halo, gathered,
     in_sem, halo_send, halo_recv, send_sem, recv_sem,
 ):
     gx, gy = lax.axis_index("gx"), lax.axis_index("gy")
@@ -58,15 +58,13 @@
         return (y_ * 2 + c_, z_ * 2 + x_)
 
     def slot(y_, c_, z_, x_):
-        return (y_ * 2 + c_) * ny + z_ * 2 + x_
-
-    after = lax.rem(me + 1, devices)
-    before = lax.rem(me + devices - 1, devices)
-    dev_after = (after // ny, lax.rem(after, ny))
-    dev_before = (before // ny, lax.rem(before, ny))
-    z_peers = [lax.rem(z + k, zs) for k in range(1, zs)]
+        return (y_ * 2 + c_) * ny + z_ * 2 + 1 - x_
+
+    by_distance = [sorted(range(zs), key=lambda q, a=a: (abs(q - a), q)) for a in range(zs)]
+    line = [sum(jnp.where(z == a, by_distance[a][k], 0) for a in range(zs)) for k in range(zs)]
     dev_x, dev_y, dev_c = dev(y, c, z, 1 - x), dev(1 - y, c, z, x), dev(y, 1 - c, z, x)
-    partners = [dev(y, c, q, x) for q in z_peers] + [dev_x, dev_y, dev_c, dev_after, dev_before]
+    dev_d = dev(1 - y, c, z, 1 - x)
+    partners = [dev(y, c, q, x) for q in line[1:]] + [dev_x, dev_y, dev_d, dev_c]
     barrier = pltpu.get_barrier_semaphore()
     for partner in partners:
         pl.semaphore_signal(barrier, inc=1, device_id=partner, device_id_type=MESH)
@@ -99,69 +97,103 @@
     mid = jnp.where(lane < LANES - ROWS, pltpu.roll(first, LANES - ROWS, 1), pltpu.roll(second, LANES - ROWS, 1))
     last = pltpu.roll(second, 2 * LANES - 2 * ROWS, 1)
     table = (first + mid + last) * scale
-    own = pack(table[:PFT_PAD])
+    own[...] = pack(table[:PFT_PAD])
     nxt[...] = pack(table[PFT_PAD:])
 
+    @pl.when((x == 1) & (z == zs - 1))
+    def _():
+        gathered[pl.ds(pl.multiple_of((REGION + gx) * MAIN, 8), MAIN), :] = nxt[...]
+
+
     pl.semaphore_wait(barrier, len(partners))
-    halo_copy = pltpu.make_async_remote_copy(
-        src_ref=nxt, dst_ref=halo, send_sem=halo_send, recv_sem=halo_recv,
-        device_id=dev_after, device_id_type=MESH,
-    )
-    halo_copy.start()
-    halo_copy.wait_recv()
-
     def chunk(s):
         return gathered.at[pl.ds(pl.multiple_of(s * MAIN, 8), MAIN), :]
 
-    gathered[pl.ds(pl.multiple_of(me * MAIN, 8), MAIN), :] = own + halo[...]
+    swap = pltpu.make_async_remote_copy(
+        src_ref=own, dst_ref=theirs, send_sem=halo_send.at[0], recv_sem=halo_recv.at[0],
+        device_id=dev_x, device_id_type=MESH,
+    )
+    shift = pltpu.make_async_remote_copy(
+        src_ref=nxt, dst_ref=halo, send_sem=halo_send.at[1], recv_sem=halo_recv.at[1],
+        device_id=dev(y, c, lax.rem(z + 1, zs), x), device_id_type=MESH,
+    )
+    shifts = (x == 1) & (z < zs - 1)
+    shifted = (x == 1) & (z > 0)
+    swap.start()
+
+    @pl.when(shifts)
+    def _():
+        shift.start()
+
+    swap.wait_recv()
+    mine = pl.ds(pl.multiple_of(slot(y, c, z, x) * MAIN, 8), MAIN)
+
+    @pl.when(x == 0)
+    def _():
+        gathered[mine, :] = theirs[...] + nxt[...]
+
+    @pl.when((x == 1) & (z == 0))
+    def _():
+        gathered[mine, :] = theirs[...]
+
+    @pl.when(shifted)
+    def _():
+        shift.wait_recv()
+        gathered[mine, :] = theirs[...] + halo[...]
+
     sent = []
 
-    def send(s, target):
-        copy = pltpu.make_async_remote_copy(
-            src_ref=chunk(s), dst_ref=chunk(s), send_sem=send_sem.at[len(sent)],
+    def copy_of(s, target, sem):
+        return pltpu.make_async_remote_copy(
+            src_ref=chunk(s), dst_ref=chunk(s), send_sem=send_sem.at[sem],
             recv_sem=recv_sem.at[s], device_id=target, device_id_type=MESH,
         )
-        copy.start()
-        sent.append(copy)
-
-    def arrive(s):
-        pltpu.make_async_remote_copy(
-            src_ref=chunk(s), dst_ref=chunk(s), send_sem=send_sem.at[0],
-            recv_sem=recv_sem.at[s], device_id=dev_x, device_id_type=MESH,
-        ).wait_recv()
-
-    send(me, dev_y)
-    send(me, dev_x)
-    for q in z_peers:
-        send(me, dev(y, c, q, x))
-    send(me, dev_c)
-    for q in z_peers:
-        s = slot(y, c, q, x)
-        arrive(s)
-        send(s, dev_y)
-        send(s, dev_x)
-        send(s, dev_c)
-    for k, q in enumerate([z] + z_peers):
-        s = slot(y, c, q, 1 - x)
-        arrive(s)
-        if k % 2 == 0:
-            send(s, dev_y)
-        send(s, dev_c)
-        s = slot(1 - y, c, q, x)
-        arrive(s)
-        if k % 2 == 1:
-            send(s, dev_x)
-        send(s, dev_c)
-    for q in [z] + z_peers:
-        s = slot(1 - y, c, q, 1 - x)
-        arrive(s)
-        send(s, dev_c)
-    for q in [z] + z_peers:
+
+    def relay(owner, targets, arrives=True):
+        y_, c_, z_, x_ = owner
+        s, e = slot(y_, c_, z_, x_), REGION + y_ * 2 + c_
+        edge = (z_ == zs - 1) & (x_ == 1)
+        sems = [len(sent) + k for k in range(len(targets))]
+        if arrives:
+            copy_of(s, dev_x, 0).wait_recv()
+        for target, sem in zip(targets, sems):
+            copy_of(s, target, 2 * sem).start()
+
+        @pl.when(edge)
+        def _():
+            if arrives:
+                copy_of(e, dev_x, 0).wait_recv()
+            for target, sem in zip(targets, sems):
+                copy_of(e, target, 2 * sem + 1).start()
+
+        sent.extend((s, e, edge, target, sem) for target, sem in zip(targets, sems))
+
+    quad = [dev_d, dev_x, dev_y]
+    relay((y, c, z, x), [dev(y, c, q, x) for q in line[:0:-1]] + quad + [dev_c], False)
+    for q in line[1:]:
+        relay((y, c, q, x), quad + [dev_c])
+    for q in line:
+        for y_, x_ in ((y, 1 - x), (1 - y, x), (1 - y, 1 - x)):
+            relay((y_, c, q, x_), [dev_c])
+    for q in line:
         for y_, x_ in ((y, x), (y, 1 - x), (1 - y, x), (1 - y, 1 - x)):
-            arrive(slot(y_, 1 - c, q, x_))
-    halo_copy.wait_send()
-    for copy in sent:
-        copy.wait_send()
+            relay((y_, 1 - c, q, x_), [])
+    swap.wait_send()
+
+    @pl.when(shifts)
+    def _():
+        shift.wait_send()
+
+    for s, e, edge, target, sem in sent:
+        copy_of(s, target, 2 * sem).wait_send()
+
+        @pl.when(edge)
+        def _(e=e, target=target, sem=sem):
+            copy_of(e, target, 2 * sem + 1).wait_send()
+
+    for g in range(2 * ys):
+        first_row = pl.ds(((g + 1) % (2 * ys)) * ny * MAIN, MAIN)
+        gathered[first_row, :] = gathered[first_row, :] + gathered[pl.ds((REGION + g) * MAIN, MAIN), :]
 
     for u in range(MAIN // 4):
         rows = [gathered[pl.ds(4 * u + j, REGION, stride=MAIN), :] for j in range(4)]
@@ -186,7 +218,7 @@
     scale = CELLS / (patches * devices)
     out = jax.ShapeDtypeStruct((POOLS, CELLS), jnp.float32)
     hbm, vmem = pl.BlockSpec(memory_space=pl.ANY), pl.BlockSpec(memory_space=pltpu.VMEM)
-    sends = 3 + zs - 1 + 3 * (zs - 1) + 3 * zs + zs
+    sends = zs - 1 + 4 * zs + 3 * zs
     return pl.pallas_call(
         functools.partial(kernel, zs, ys, scale),
         out_shape=(out, out),
@@ -198,12 +230,14 @@
             pltpu.VMEM((POOLS, patches), jnp.float32),
             pltpu.VMEM((MAIN, LANES), jnp.float32),
             pltpu.VMEM((MAIN, LANES), jnp.float32),
-            pltpu.VMEM((REGION * MAIN, LANES), jnp.float32),
+            pltpu.VMEM((MAIN, LANES), jnp.float32),
+            pltpu.VMEM((MAIN, LANES), jnp.float32),
+            pltpu.VMEM(((REGION + 2 * ys) * MAIN, LANES), jnp.float32),
             pltpu.SemaphoreType.DMA((3, BLOCKS)),
-            pltpu.SemaphoreType.DMA,
-            pltpu.SemaphoreType.DMA,
-            pltpu.SemaphoreType.DMA((sends,)),
-            pltpu.SemaphoreType.DMA((devices,)),
+            pltpu.SemaphoreType.DMA((2,)),
+            pltpu.SemaphoreType.DMA((2,)),
+            pltpu.SemaphoreType.DMA((2 * sends,)),
+            pltpu.SemaphoreType.DMA((devices + 2 * ys,)),
         ],
         compiler_params=pltpu.CompilerParams(collective_id=0, has_side_effects=True),
     )(pool_old, pool_new, flux, area[None, :], pft_id[None, :], region_id[None, :])

time: 26.8 us -> 25 us (0.933)
  the two profiles are of different devices: /device:TPU:27 before, /device:TPU:0 now
where the time goes in v2:
time: 25 us; the launch traced here: 24.7 us
  Pallas kernels  21.5 us (86%)
  local copies, waits for them, and re-layouts  2.59 us (10%)
  between operations  0.65 us (3%)
    pallas_call x1, Pallas kernels, kernel_shards(): pl.pallas_call(functools.partial(kernel, zs, ys, scale), out_shape=(out,...  21.5 us
    unnamed x4, local copies, waits for them, and re-layouts  2.59 us

profile of v2, /device:TPU:0, one launch (start us, length us, event | category | flops | bytes accessed | tf_op | source)
XLA Modules:
  0.0 24.7 jit_solution(6471047414820001902)
XLA Ops:
  0.6 21.5 %shard_map.77 = (f32[40,2528]{1,0:T(8,128)}, f32[40,2528]{1,0:T(8,128)}) custom-call(f32[40,4096]{1,0:T(8,128)} %old_hbm.1, f32[40,4096]{1,0:T(8,128)} %new_hbm.1, f32[40,4096]{1,0:T(8,128)} %flux_hbm.1, f32[1,4096]{1,0:T(1,128)} %bitcast.3, s32[1,4096]{1,0:T(1,128)} %bitcast.4, s32[1,4096]{1,0:T(1,128)} %bitcast.5), custom_call_target="tpu_custom_call" | custom-call | tf_op jit(solution)/shard_map/pallas_call | solution.py:222
  22.1 0.0 copy-start
  22.1 1.8 %copy.10 = f32[40,2528]{1,0:T(8,128)} copy(f32[40,2528]{1,0:T(8,128)} %get-tuple-element.4) | data formatting | bytes 808960
  23.9 0.0 copy-done
  24.0 0.8 %copy.11 = f32[40,2528]{1,0:T(8,128)} copy(f32[40,2528]{1,0:T(8,128)S(1)} %copy-done) | data formatting | bytes 808960
Async XLA Ops:
  22.1 1.8 %copy-start = (f32[40,2528]{1,0:T(8,128)S(1)}, f32[40,2528]{1,0:T(8,128)}, u32[]{:S(2)}) copy-start(f32[40,2528]{1,0:T(8,128)} %get-tuple-element.5) | copy-start | bytes 1213444

commit v3 on v2

--- a/solution.py
+++ b/solution.py
@@ -34,7 +34,7 @@
 def kernel(
     zs, ys, scale,
     old_hbm, new_hbm, flux_hbm, area_ref, pft_ref, region_ref,
-    stored_ref, error_ref,
+    out_ref,
     old_v, new_v, flux_v, own, nxt, theirs, halo, gathered,
     in_sem, halo_send, halo_recv, send_sem, recv_sem,
 ):
@@ -199,31 +199,29 @@
         rows = [gathered[pl.ds(4 * u + j, REGION, stride=MAIN), :] for j in range(4)]
         tile = jnp.concatenate(rows, axis=0).T
         here = pl.ds(u * LANES, LANES)
-        stored_ref[:, here] = tile[:POOLS]
-        error_ref[:, here] = tile[POOLS:ROWS]
+        out_ref[:, here] = tile[:ROWS]
         if 4 * u < 2 * REST:
             t = (MAIN // 4) + (u if 4 * u < REST else u - REST // 4)
             w = min(LANES, CELLS - t * LANES)
             there = pl.ds(t * LANES, w)
             if 4 * u < REST:
-                stored_ref[:, there] = tile[ROWS : ROWS + POOLS, :w]
-                error_ref[: SPARE - POOLS, there] = tile[ROWS + POOLS :, :w]
+                out_ref[:SPARE, there] = tile[ROWS:, :w]
             else:
-                error_ref[SPARE - POOLS :, there] = tile[ROWS : 2 * ROWS - SPARE, :w]
+                out_ref[SPARE:, there] = tile[ROWS : 2 * ROWS - SPARE, :w]
 
 
 def kernel_shards(zs, ys, pool_old, pool_new, flux, area, pft_id, region_id):
     patches = area.shape[0]
     devices = 4 * ys * zs
     scale = CELLS / (patches * devices)
-    out = jax.ShapeDtypeStruct((POOLS, CELLS), jnp.float32)
+    out = jax.ShapeDtypeStruct((ROWS, CELLS), jnp.float32)
     hbm, vmem = pl.BlockSpec(memory_space=pl.ANY), pl.BlockSpec(memory_space=pltpu.VMEM)
     sends = zs - 1 + 4 * zs + 3 * zs
-    return pl.pallas_call(
+    both = pl.pallas_call(
         functools.partial(kernel, zs, ys, scale),
-        out_shape=(out, out),
+        out_shape=out,
         in_specs=[hbm] * 3 + [vmem] * 3,
-        out_specs=(vmem, vmem),
+        out_specs=vmem,
         scratch_shapes=[
             pltpu.VMEM((POOLS, patches), jnp.float32),
             pltpu.VMEM((POOLS, patches), jnp.float32),
@@ -241,6 +239,7 @@
         ],
         compiler_params=pltpu.CompilerParams(collective_id=0, has_side_effects=True),
     )(pool_old, pool_new, flux, area[None, :], pft_id[None, :], region_id[None, :])
+    return (both[:POOLS], both[POOLS:])
 
 
 def shards(pool_old, pool_new, flux, area, pft_id, region_id):

time: 25 us -> 24.5 us (0.980)
  local copies, waits for them, and re-layouts: 2.59 us -> 2.08 us
    unnamed x4 -> x0, local copies, waits for them, and re-layouts: 2.59 us -> none
    slice x0 -> x1, local copies, waits for them, and re-layouts: none -> 2.08 us  [kernel_shards(): return (both[:POOLS], both[POOLS:])]
where the time goes in v3:
time: 24.5 us; the launch traced here: 24.2 us
  Pallas kernels  21.5 us (88%)
  local copies, waits for them, and re-layouts  2.08 us (8%)
  between operations  0.64 us (3%)
    pallas_call x1, Pallas kernels, kernel_shards(): pl.pallas_call(functools.partial(kernel, zs, ys, scale), out_shape=out, i...  21.5 us
    slice x1, local copies, waits for them, and re-layouts, kernel_shards(): return (both[:POOLS], both[POOLS:])  2.08 us

profile of v3, /device:TPU:0, one launch (start us, length us, event | category | flops | bytes accessed | tf_op | source)
XLA Modules:
  0.0 24.2 jit_solution(827966307690275986)
XLA Ops:
  0.6 21.5 %shard_map.77 = f32[80,2528]{1,0:T(8,128)} custom-call(f32[40,4096]{1,0:T(8,128)} %old_hbm.1, f32[40,4096]{1,0:T(8,128)} %new_hbm.1, f32[40,4096]{1,0:T(8,128)} %flux_hbm.1, f32[1,4096]{1,0:T(1,128)} %bitcast.3, s32[1,4096]{1,0:T(1,128)} %bitcast.4, s32[1,4096]{1,0:T(1,128)} %bitcast.5), custom_call_target="tpu_custom_call" | custom-call | tf_op jit(solution)/shard_map/pallas_call | solution.py:220
  22.1 2.1 %fusion = (f32[40,2528]{1,0:T(8,128)}, f32[40,2528]{1,0:T(8,128)}) fusion(f32[80,2528]{1,0:T(8,128)} %shard_map.77), kind=kLoop, calls=%fused_computation | loop fusion | bytes 1617920 | tf_op jit(solution)/shard_map/slice | solution.py:242
